TPU v7x, 256 devices: a whole 4x4x8 slice. The times are simulated.
256 devices in a mesh: grp: 16 (over z, core), row: 16 (over y, x).
Axes of the slice: x: 4, y: 4, z: 8, core: 2. Of those that a mesh axis runs over, the one named last changes fastest.
Arguments:
- theta: float32 [32, 512, 512], P('grp', 'row'), may hold values from -8 to 8
- left_env: bfloat16 [32, 8, 512, 512], P('grp', None, 'row'), may hold values from -1.5 to 1.5
- right_env: bfloat16 [32, 8, 512, 512], P('grp', None, 'row'), may hold values from -3.5 to 3.5
- lengths: int32 [32, 2], P('grp'), may hold values from 128 to 512
Outputs:
- evolved: float32 [32, 512, 512], P('grp', 'row')
- hessenberg: float32 [8, 8], replicated
All inputs are finite; a program needn't handle non-finite values.
Results may differ from a plain program's by a relative error of at most 0.0029.
Values may be sent and summed in bfloat16 or wider, within the bound.
No kernel may reach another device: no remote copies, remote signals or barrier semaphores. Data moves between devices by JAX's collectives and lax.ppermute only.
A program may use at most 64 MiB of HBM per device.

v0:
```python
import functools
import jax
import jax.numpy as jnp
from jax import lax
from jax.sharding import Mesh
from jax.sharding import PartitionSpec as P

KRYLOV = 8
ROW = ("row_0", "row_1")
GRP_ROW = ("grp_0", "grp_1", "row_0", "row_1")
GRP = ("grp_0", "grp_1")
epsilon = 1e-06
time_step = 0.5


def split_up(value, dim, length):
    dims = value.shape
    tiles = value.reshape(*dims[:dim], length, dims[dim] // length, *dims[dim + 1 :])
    return jnp.moveaxis(tiles, dim, 0)


def sent_and_summed(value, axis, dim):
    tiles = split_up(value, dim, lax.axis_size(axis))
    arrived = lax.all_to_all(tiles, axis, split_axis=0, concat_axis=0, tiled=True)
    return arrived.sum(axis=0)


def over_axes(value, axes):
    return functools.reduce(lax.psum, axes, value)


def propagate(hessenberg):
    krylov_size = hessenberg.shape[0]
    scaled = time_step * hessenberg
    series = jnp.eye(krylov_size, dtype=jnp.float32)
    series_term = jnp.eye(krylov_size, dtype=jnp.float32)
    for degree in range(1, 19):
        series_term = jnp.dot(series_term, scaled, precision=lax.Precision.HIGHEST) / degree
        series = series + series_term
    return series[:, 0]


def local(theta, left_env, right_env, lengths):
    local_rows = theta.shape[1]
    sect_width = theta.shape[2]
    row_start = lax.axis_index(ROW) * local_rows
    row_ids = row_start + lax.broadcasted_iota(jnp.int32, (1, local_rows, 1), 1)
    col_ids = lax.broadcasted_iota(jnp.int32, (1, 1, sect_width), 2)
    live_mask = (
        (row_ids < lengths[:, 0][:, None, None]) & (col_ids < lengths[:, 1][:, None, None])
    ).astype(jnp.float32)
    right_full = lax.all_gather(right_env, ROW, axis=2, tiled=True)
    start_block = theta * live_mask
    norm_zero = jnp.sqrt(over_axes(jnp.sum(start_block * start_block), GRP_ROW) + epsilon)
    krylov_basis = [start_block / norm_zero]
    krylov_size = KRYLOV
    hessenberg = jnp.zeros((krylov_size, krylov_size), jnp.float32)
    for column in range(krylov_size):
        packed = krylov_basis[column].astype(jnp.bfloat16)
        inner_terms = jnp.einsum(
            "sab,swbc->swac", packed, right_full, preferred_element_type=jnp.float32
        )
        inner_terms = inner_terms.astype(jnp.bfloat16)
        partial_image = jnp.einsum(
            "swba,swbc->sac", left_env, inner_terms, preferred_element_type=jnp.float32
        )
        image = sent_and_summed(partial_image, ROW, 1) * live_mask
        local_dots = jnp.stack([jnp.sum(vector * image) for vector in krylov_basis])
        coefficients, squared = (
            over_axes(local_dots, GRP_ROW),
            over_axes(jnp.sum(image * image), GRP_ROW),
        )
        for previous in range(column + 1):
            image = image - coefficients[previous] * krylov_basis[previous]
        hessenberg = hessenberg.at[: column + 1, column].set(coefficients)
        if column + 1 < krylov_size:
            beta_norm = jnp.sqrt(squared - jnp.sum(coefficients * coefficients) + epsilon)
            hessenberg = hessenberg.at[column + 1, column].set(beta_norm)
            krylov_basis.append(image / beta_norm)
    weights = propagate(hessenberg)
    evolved = jnp.zeros_like(start_block)
    for column in range(krylov_size):
        evolved = evolved + weights[column] * krylov_basis[column]
    return (norm_zero * evolved, hessenberg)


def solution(mesh):
    finer = Mesh(mesh.devices.reshape(8, 2, 4, 4), ("grp_0", "grp_1", "row_0", "row_1"))
    return jax.shard_map(
        local,
        mesh=finer,
        in_specs=(
            P(GRP, ROW, None),
            P(GRP, None, ROW, None),
            P(GRP, None, ROW, None),
            P(GRP, None),
        ),
        out_specs=(P(GRP, ROW, None), P()),
        check_vma=False,
    )
```

profile of v0, /device:TPU:32, one launch (start us, length us, event | category | flops | bytes accessed | tf_op | source)
XLA Modules:
  0.0 776.2 jit_solution(253862596949875197)
XLA Ops:
  10.7 18.5 %psum.448 = f32[]{:T(128)} all-reduce(f32[]{:T(128)} %multiply_reduce_fusion.43), channel_id=1, replica_groups=mesh['grp_0'=8,'grp_1'=2,'row_0'=4,'row_1'=4] {'grp_0'}, use_global_device_ids=true, to_apply=%region_1.0 | all-reduce | flops 1 | bytes 8 | tf_op jit(solution)/shard_map/psum | solution.py:29
  32.2 11.3 %psum.450 = f32[]{:T(128)} all-reduce(f32[]{:T(128)} %psum.449), channel_id=1, replica_groups=mesh['grp_0'=8,'grp_1'=2,'row_0'=4,'row_1'=4] {'row_0'}, use_global_device_ids=true, to_apply=%region_3.0 | all-reduce | flops 1 | bytes 8 | tf_op jit(solution)/shard_map/psum | solution.py:29
  43.6 11.1 %psum.451 = f32[]{:T(128)} all-reduce(f32[]{:T(128)} %psum.450), channel_id=1, replica_groups=mesh['grp_0'=8,'grp_1'=2,'row_0'=4,'row_1'=4] {'row_1'}, use_global_device_ids=true, to_apply=%region_4.0 | all-reduce | flops 1 | bytes 8 | tf_op jit(solution)/shard_map/psum | solution.py:29
  55.4 33.5 %all-gather.2.cloned.1.call-done = bf16[2,8,512,512]{3,2,1,0:T(8,128)(2,1)} async-done(((bf16[2,8,32,512]{3,2,1,0:T(8,128)(2,1)}), bf16[2,8,512,512]{3,2,1,0:T(8,128)(2,1)}) %all-gather.2.cloned.1.call-update) | async-done | bytes 8388624 | tf_op jit(solution)/shard_map/all_gather | solution.py:52
  94.5 33.3 %all_to_all.40 = f32[16,2,32,512]{3,2,1,0:T(8,128)S(1)} all-to-all(f32[16,2,32,512]{3,2,1,0:T(8,128)S(1)} %bitcast.287), channel_id=1, replica_groups=mesh['grp_0'=8,'grp_1'=2,'row_0'=4,'row_1'=4] {'row_0','row_1'}, dimensions={0} | all-to-all | bytes 4194304 | tf_op jit(solution)/shard_map/all_to_all | solution.py:24
  128.7 16.7 %all-reduce.7 = (f32[]{:T(128)}, f32[1]{0:T(128)}) all-reduce(f32[]{:T(128)} %get-tuple-element.224, f32[1]{0:T(128)} %bitcast.8), channel_id=1, replica_groups=mesh['grp_0'=8,'grp_1'=2,'row_0'=4,'row_1'=4] {'grp_0'}, use_global_device_ids=true, to_apply=%region_12.0 | all-reduce | flops 2 | bytes 16 | tf_op jit(solution)/shard_map/psum | solution.py:29
  148.5 9.2 %all-reduce.21 = (f32[]{:T(128)}, f32[1]{0:T(128)}) all-reduce(f32[]{:T(128)} %get-tuple-element.281, f32[1]{0:T(128)} %get-tuple-element.282), channel_id=1, replica_groups=mesh['grp_0'=8,'grp_1'=2,'row_0'=4,'row_1'=4] {'row_0'}, use_global_device_ids=true, to_apply=%region_14.0 | all-reduce | flops 2 | bytes 16 | tf_op jit(solution)/shard_map/psum | solution.py:29
  157.6 9.2 %all-reduce.14 = (f32[]{:T(128)}, f32[1]{0:T(128)}) all-reduce(f32[]{:T(128)} %get-tuple-element.267, f32[1]{0:T(128)} %get-tuple-element.268), channel_id=1, replica_groups=mesh['grp_0'=8,'grp_1'=2,'row_0'=4,'row_1'=4] {'row_1'}, use_global_device_ids=true, to_apply=%region_15.0 | all-reduce | flops 2 | bytes 16 | tf_op jit(solution)/shard_map/psum | solution.py:29
  175.1 27.9 %all_to_all.41 = f32[16,2,32,512]{3,2,1,0:T(8,128)S(1)} all-to-all(f32[16,2,32,512]{3,2,1,0:T(8,128)S(1)} %bitcast.288), channel_id=1, replica_groups=mesh['grp_0'=8,'grp_1'=2,'row_0'=4,'row_1'=4] {'row_0','row_1'}, dimensions={0} | all-to-all | bytes 4194304 | tf_op jit(solution)/shard_map/all_to_all | solution.py:24
  205.2 16.6 %all-reduce.6 = (f32[]{:T(128)}, f32[2]{0:T(128)S(1)}) all-reduce(f32[]{:T(128)} %get-tuple-element.222, f32[2]{0:T(128)S(1)} %pad_maximum_fusion), channel_id=1, replica_groups=mesh['grp_0'=8,'grp_1'=2,'row_0'=4,'row_1'=4] {'grp_0'}, use_global_device_ids=true, to_apply=%region_24.0 | all-reduce | flops 3 | bytes 24 | tf_op jit(solution)/shard_map/psum | solution.py:29
  224.9 9.2 %all-reduce.20 = (f32[]{:T(128)}, f32[2]{0:T(128)S(1)}) all-reduce(f32[]{:T(128)} %get-tuple-element.279, f32[2]{0:T(128)S(1)} %get-tuple-element.280), channel_id=1, replica_groups=mesh['grp_0'=8,'grp_1'=2,'row_0'=4,'row_1'=4] {'row_0'}, use_global_device_ids=true, to_apply=%region_26.0 | all-reduce | flops 3 | bytes 24 | tf_op jit(solution)/shard_map/psum | solution.py:29
  234.1 9.2 %all-reduce.13 = (f32[]{:T(128)}, f32[2]{0:T(128)S(1)}) all-reduce(f32[]{:T(128)} %get-tuple-element.265, f32[2]{0:T(128)S(1)} %get-tuple-element.266), channel_id=1, replica_groups=mesh['grp_0'=8,'grp_1'=2,'row_0'=4,'row_1'=4] {'row_1'}, use_global_device_ids=true, to_apply=%region_27.0 | all-reduce | flops 3 | bytes 24 | tf_op jit(solution)/shard_map/psum | solution.py:29
  252.6 27.9 %all_to_all.42 = f32[16,2,32,512]{3,2,1,0:T(8,128)S(1)} all-to-all(f32[16,2,32,512]{3,2,1,0:T(8,128)S(1)} %bitcast.289), channel_id=1, replica_groups=mesh['grp_0'=8,'grp_1'=2,'row_0'=4,'row_1'=4] {'row_0','row_1'}, dimensions={0} | all-to-all | bytes 4194304 | tf_op jit(solution)/shard_map/all_to_all | solution.py:24
  283.2 15.6 %all-reduce.5 = (f32[]{:T(128)}, f32[3]{0:T(128)S(1)}) all-reduce(f32[]{:T(128)} %get-tuple-element.219, f32[3]{0:T(128)S(1)} %pad_maximum_fusion.1), channel_id=1, replica_groups=mesh['grp_0'=8,'grp_1'=2,'row_0'=4,'row_1'=4] {'grp_0'}, use_global_device_ids=true, to_apply=%region_39.0 | all-reduce | flops 4 | bytes 32 | tf_op jit(solution)/shard_map/psum | solution.py:29
  302.0 9.2 %all-reduce.19 = (f32[]{:T(128)}, f32[3]{0:T(128)S(1)}) all-reduce(f32[]{:T(128)} %get-tuple-element.277, f32[3]{0:T(128)S(1)} %get-tuple-element.278), channel_id=1, replica_groups=mesh['grp_0'=8,'grp_1'=2,'row_0'=4,'row_1'=4] {'row_0'}, use_global_device_ids=true, to_apply=%region_41.0 | all-reduce | flops 4 | bytes 32 | tf_op jit(solution)/shard_map/psum | solution.py:29
  311.2 9.2 %all-reduce.12 = (f32[]{:T(128)}, f32[3]{0:T(128)S(1)}) all-reduce(f32[]{:T(128)} %get-tuple-element.263, f32[3]{0:T(128)S(1)} %get-tuple-element.264), channel_id=1, replica_groups=mesh['grp_0'=8,'grp_1'=2,'row_0'=4,'row_1'=4] {'row_1'}, use_global_device_ids=true, to_apply=%region_42.0 | all-reduce | flops 4 | bytes 32 | tf_op jit(solution)/shard_map/psum | solution.py:29
  330.3 27.9 %all_to_all.43 = f32[16,2,32,512]{3,2,1,0:T(8,128)S(1)} all-to-all(f32[16,2,32,512]{3,2,1,0:T(8,128)S(1)} %bitcast.290), channel_id=1, replica_groups=mesh['grp_0'=8,'grp_1'=2,'row_0'=4,'row_1'=4] {'row_0','row_1'}, dimensions={0} | all-to-all | bytes 4194304 | tf_op jit(solution)/shard_map/all_to_all | solution.py:24
  361.6 15.9 %all-reduce.4 = (f32[]{:T(128)}, f32[4]{0:T(128)S(1)}) all-reduce(f32[]{:T(128)} %get-tuple-element.215, f32[4]{0:T(128)S(1)} %pad_maximum_fusion.2), channel_id=1, replica_groups=mesh['grp_0'=8,'grp_1'=2,'row_0'=4,'row_1'=4] {'grp_0'}, use_global_device_ids=true, to_apply=%region_55.0 | all-reduce | flops 5 | bytes 40 | tf_op jit(solution)/shard_map/psum | solution.py:29
  380.6 9.2 %all-reduce.18 = (f32[]{:T(128)}, f32[4]{0:T(128)S(1)}) all-reduce(f32[]{:T(128)} %get-tuple-element.275, f32[4]{0:T(128)S(1)} %get-tuple-element.276), channel_id=1, replica_groups=mesh['grp_0'=8,'grp_1'=2,'row_0'=4,'row_1'=4] {'row_0'}, use_global_device_ids=true, to_apply=%region_57.0 | all-reduce | flops 5 | bytes 40 | tf_op jit(solution)/shard_map/psum | solution.py:29
  389.7 9.4 %all-reduce.11 = (f32[]{:T(128)}, f32[4]{0:T(128)S(1)}) all-reduce(f32[]{:T(128)} %get-tuple-element.261, f32[4]{0:T(128)S(1)} %get-tuple-element.262), channel_id=1, replica_groups=mesh['grp_0'=8,'grp_1'=2,'row_0'=4,'row_1'=4] {'row_1'}, use_global_device_ids=true, to_apply=%region_58.0 | all-reduce | flops 5 | bytes 40 | tf_op jit(solution)/shard_map/psum | solution.py:29
  409.6 27.9 %all_to_all.44 = f32[16,2,32,512]{3,2,1,0:T(8,128)S(1)} all-to-all(f32[16,2,32,512]{3,2,1,0:T(8,128)S(1)} %bitcast.291), channel_id=1, replica_groups=mesh['grp_0'=8,'grp_1'=2,'row_0'=4,'row_1'=4] {'row_0','row_1'}, dimensions={0} | all-to-all | bytes 4194304 | tf_op jit(solution)/shard_map/all_to_all | solution.py:24
  441.4 15.7 %all-reduce.3 = (f32[]{:T(128)}, f32[5]{0:T(128)S(1)}) all-reduce(f32[]{:T(128)} %get-tuple-element.209, f32[5]{0:T(128)S(1)} %stack.147), channel_id=1, replica_groups=mesh['grp_0'=8,'grp_1'=2,'row_0'=4,'row_1'=4] {'grp_0'}, use_global_device_ids=true, to_apply=%region_72.0 | all-reduce | flops 6 | bytes 48 | tf_op jit(solution)/shard_map/psum | solution.py:29
  460.1 9.2 %all-reduce.17 = (f32[]{:T(128)}, f32[5]{0:T(128)S(1)}) all-reduce(f32[]{:T(128)} %get-tuple-element.273, f32[5]{0:T(128)S(1)} %get-tuple-element.274), channel_id=1, replica_groups=mesh['grp_0'=8,'grp_1'=2,'row_0'=4,'row_1'=4] {'row_0'}, use_global_device_ids=true, to_apply=%region_74.0 | all-reduce | flops 6 | bytes 48 | tf_op jit(solution)/shard_map/psum | solution.py:29
  469.3 9.2 %all-reduce.10 = (f32[]{:T(128)}, f32[5]{0:T(128)S(1)}) all-reduce(f32[]{:T(128)} %get-tuple-element.259, f32[5]{0:T(128)S(1)} %get-tuple-element.260), channel_id=1, replica_groups=mesh['grp_0'=8,'grp_1'=2,'row_0'=4,'row_1'=4] {'row_1'}, use_global_device_ids=true, to_apply=%region_75.0 | all-reduce | flops 6 | bytes 48 | tf_op jit(solution)/shard_map/psum | solution.py:29
  489.7 27.9 %all_to_all.45 = f32[16,2,32,512]{3,2,1,0:T(8,128)S(1)} all-to-all(f32[16,2,32,512]{3,2,1,0:T(8,128)S(1)} %bitcast.292), channel_id=1, replica_groups=mesh['grp_0'=8,'grp_1'=2,'row_0'=4,'row_1'=4] {'row_0','row_1'}, dimensions={0} | all-to-all | bytes 4194304 | tf_op jit(solution)/shard_map/all_to_all | solution.py:24
  522.4 15.9 %all-reduce.2 = (f32[]{:T(128)}, f32[6]{0:T(128)S(1)}) all-reduce(f32[]{:T(128)} %get-tuple-element.203, f32[6]{0:T(128)S(1)} %stack.154), channel_id=1, replica_groups=mesh['grp_0'=8,'grp_1'=2,'row_0'=4,'row_1'=4] {'grp_0'}, use_global_device_ids=true, to_apply=%region_90.0 | all-reduce | flops 7 | bytes 56 | tf_op jit(solution)/shard_map/psum | solution.py:29
  550.5 9.2 %all-reduce.9 = (f32[]{:T(128)}, f32[6]{0:T(128)S(1)}) all-reduce(f32[]{:T(128)} %get-tuple-element.257, f32[6]{0:T(128)S(1)} %get-tuple-element.258), channel_id=1, replica_groups=mesh['grp_0'=8,'grp_1'=2,'row_0'=4,'row_1'=4] {'row_1'}, use_global_device_ids=true, to_apply=%region_93.0 | all-reduce | flops 7 | bytes 56 | tf_op jit(solution)/shard_map/psum | solution.py:29
  579.3 24.5 %all-to-all-done.6 = f32[16,2,32,512]{3,2,1,0:T(8,128)S(1)} async-done(((f32[16,2,32,512]{3,2,1,0:T(8,128)}), f32[16,2,32,512]{3,2,1,0:T(8,128)S(1)}, u32[]{:S(2)}, u32[]{:S(2)}) %all-to-all-start.6) | async-done | bytes 2097184 | tf_op jit(solution)/shard_map/all_to_all | solution.py:24
  610.7 15.7 %all-reduce.1 = (f32[]{:T(128)}, f32[7]{0:T(128)S(1)}) all-reduce(f32[]{:T(128)} %get-tuple-element.196, f32[7]{0:T(128)S(1)} %stack.162), channel_id=1, replica_groups=mesh['grp_0'=8,'grp_1'=2,'row_0'=4,'row_1'=4] {'grp_0'}, use_global_device_ids=true, to_apply=%region_109.0 | all-reduce | flops 8 | bytes 64 | tf_op jit(solution)/shard_map/psum | solution.py:29
  717.0 15.3 %psum.508 = f32[8]{0:T(128)S(1)} all-reduce(f32[8]{0:T(128)S(1)} %stack.171), channel_id=1, replica_groups=mesh['grp_0'=8,'grp_1'=2,'row_0'=4,'row_1'=4] {'grp_0'}, use_global_device_ids=true, to_apply=%region_123.0 | all-reduce | flops 8 | bytes 64 | tf_op jit(solution)/shard_map/psum | solution.py:29
  738.0 10.9 %psum.510 = f32[8]{0:T(128)S(1)} all-reduce(f32[8]{0:T(128)S(1)} %psum.509), channel_id=1, replica_groups=mesh['grp_0'=8,'grp_1'=2,'row_0'=4,'row_1'=4] {'row_0'}, use_global_device_ids=true, to_apply=%region_125.0 | all-reduce | flops 8 | bytes 64 | tf_op jit(solution)/shard_map/psum | solution.py:29
  749.0 10.4 %psum.511 = f32[8,1]{1,0:T(8,128)S(1)} all-reduce(f32[8,1]{1,0:T(8,128)S(1)} %copy.27), channel_id=1, replica_groups=mesh['grp_0'=8,'grp_1'=2,'row_0'=4,'row_1'=4] {'row_1'}, use_global_device_ids=true, to_apply=%region_126.0 | all-reduce | flops 8 | bytes 64 | tf_op jit(solution)/shard_map/psum | solution.py:29
  (160 shorter events, 229.9 us)
Async XLA Ops:
  7.2 81.7 %copy-start = (bf16[2,8,32,512]{3,2,1,0:T(8,128)(2,1)S(1)}, bf16[2,8,32,512]{3,2,1,0:T(8,128)(2,1)}, u32[]{:S(2)}) copy-start(bf16[2,8,32,512]{3,2,1,0:T(8,128)(2,1)} %param.35) | copy-start | bytes 1572868
  7.2 81.7 %all-gather.2.cloned.1.call-start = ((), (), s32[]{:S(2)}) async-start(), calls=%async_computation.8 | async-start | bytes 8912896 | tf_op jit(solution)/shard_map/all_gather | solution.py:52
  55.4 72.6 %copy-start.1 = (f32[2,32,512]{2,1,0:T(8,128)S(1)}, f32[2,32,512]{2,1,0:T(8,128)}, u32[]{:S(2)}) copy-start(f32[2,32,512]{2,1,0:T(8,128)} %param.34) | copy-start | bytes 393220
  243.3 2.5 copy-start.7
  320.4 2.5 copy-start.6
  399.1 2.4 copy-start.5
  478.5 39.0 %copy-start.4 = (f32[5]{0:T(128)}, f32[5]{0:T(128)S(1)}, u32[]{:S(2)}) copy-start(f32[5]{0:T(128)S(1)} %get-tuple-element.246) | copy-start | bytes 64
  559.8 13.0 %copy-start.3 = (f32[6]{0:T(128)}, f32[6]{0:T(128)S(1)}, u32[]{:S(2)}) copy-start(f32[6]{0:T(128)S(1)} %get-tuple-element.244) | copy-start | bytes 76
  572.8 31.0 %all-to-all-start.6 = ((f32[16,2,32,512]{3,2,1,0:T(8,128)}), f32[16,2,32,512]{3,2,1,0:T(8,128)S(1)}, u32[]{:S(2)}, u32[]{:S(2)}) async-start(f32[16,2,32,512]{3,2,1,0:T(8,128)} %bitcast.286), calls=%async_computation.6 | async-start | bytes 4194304 | tf_op jit(solution)/shard_map/all_to_all | solution.py:24
  662.5 46.6 %all-to-all-start.7 = ((f32[16,2,32,512]{3,2,1,0:T(8,128)}), f32[16,2,32,512]{3,2,1,0:T(8,128)S(1)}, u32[]{:S(2)}, u32[]{:S(2)}) async-start(f32[16,2,32,512]{3,2,1,0:T(8,128)} %bitcast.285), calls=%async_computation.7 | async-start | bytes 4194304 | tf_op jit(solution)/shard_map/all_to_all | solution.py:24
  759.6 9.8 %copy-start.2 = (f32[8,8]{1,0:T(8,128)}, f32[8,8]{1,0:T(8,128)S(1)}, u32[]{:S(2)}) copy-start(f32[8,8]{1,0:T(8,128)S(1)} %scatter.74) | copy-start | bytes 772
Sparse Core Ops, SparseCore 0:
  10.4 78.4 all-gather.1
where the time goes:
time: 779 us; the launch traced here: 776 us
  blocking collectives  517 us (66%)
  other arithmetic  70.9 us (9%)
  waiting for transfers between devices  58.6 us (8%)
  local copies, waits for them, and re-layouts  52.1 us (7%)
  matrix products  44.7 us (6%)
  between operations  24.8 us (3%)
    psum x36, blocking collectives, over_axes(): return functools.reduce(lax.psum, axes, value)  345 us
    all_to_all x6, blocking collectives, sent_and_summed(): lax.all_to_all(tiles, axis, split_axis=0, concat_axis=0, tiled=True)  173 us
    dot_general x8, matrix products, local(): jnp.einsum('swba,swbc->sac', left_env, inner_terms, preferred_element_typ...  42.2 us
    all_gather x1, waiting for transfers between devices, local(): right_full = lax.all_gather(right_env, ROW, axis=2, tiled=True)  33.5 us
    all_to_all x2, waiting for transfers between devices, sent_and_summed(): lax.all_to_all(tiles, axis, split_axis=0, concat_axis=0, tiled=True)  24.5 us
    another operation x15, other arithmetic  23.1 us
    div x7, other arithmetic, local(): krylov_basis.append(image / beta_norm)  19.2 us
    another operation x4, local copies, waits for them, and re-layouts, local(): local_dots = jnp.stack([jnp.sum(vector * image) for vector in krylov_basis])  16.3 us
  transfers between devices with their start and end apart: 3, of which 2 were waited for; matrix products, arithmetic and copies ran while one was open for 6% of the time, Pallas kernels for 0%

commit v1 on v0

--- a/solution.py
+++ b/solution.py
@@ -11,6 +11,13 @@
 GRP = ("grp_0", "grp_1")
 epsilon = 1e-06
 time_step = 0.5
+
+
+def swapped_in(x, name, dim):
+    size = lax.axis_size(name)
+    pieces = jnp.stack([x for _ in range(size)])
+    pieces = lax.all_to_all(pieces, name, split_axis=0, concat_axis=0)
+    return jnp.concatenate(pieces, axis=dim)
 
 
 def split_up(value, dim, length):
@@ -49,7 +56,7 @@
     live_mask = (
         (row_ids < lengths[:, 0][:, None, None]) & (col_ids < lengths[:, 1][:, None, None])
     ).astype(jnp.float32)
-    right_full = lax.all_gather(right_env, ROW, axis=2, tiled=True)
+    right_full = swapped_in(right_env, ROW, 2)
     start_block = theta * live_mask
     norm_zero = jnp.sqrt(over_axes(jnp.sum(start_block * start_block), GRP_ROW) + epsilon)
     krylov_basis = [start_block / norm_zero]

time: 779 us -> 833 us (1.069)
  blocking collectives: 517 us -> 599 us
  waiting for transfers between devices: 58.6 us -> 25 us
  between operations: 24.8 us -> 11.4 us
  local copies, waits for them, and re-layouts: 52.1 us -> 64.2 us
    psum x36, blocking collectives: 345 us -> 428 us  [over_axes(): return functools.reduce(lax.psum, axes, value)]
    all_gather x1 -> x0, waiting for transfers between devices: 33.5 us -> none  [local(): right_full = lax.all_gather(right_env, ROW, axis=2, tiled=True)]
    another operation x14 -> x15, local copies, waits for them, and re-layouts: 12.3 us -> 16.9 us
  transfers between devices with their start and end apart: 3 -> 3, of which waited for: 2 -> 1; matrix products, arithmetic and copies ran while one was open for 6% -> 5% of each run, Pallas kernels for 0% -> 0%
where the time goes in v1:
time: 833 us; the launch traced here: 830 us
  blocking collectives  599 us (72%)
  other arithmetic  70.4 us (8%)
  local copies, waits for them, and re-layouts  64.2 us (8%)
  matrix products  44.7 us (5%)
  waiting for transfers between devices  25 us (3%)
  starting transfers between devices  14.9 us (2%)
  between operations  11.4 us (1%)
    psum x36, blocking collectives, over_axes(): return functools.reduce(lax.psum, axes, value)  428 us
    all_to_all x6, blocking collectives, sent_and_summed(): lax.all_to_all(tiles, axis, split_axis=0, concat_axis=0, tiled=True)  171 us
    dot_general x8, matrix products, local(): jnp.einsum('swba,swbc->sac', left_env, inner_terms, preferred_element_typ...  42.2 us
    all_to_all x2, waiting for transfers between devices, sent_and_summed(): lax.all_to_all(tiles, axis, split_axis=0, concat_axis=0, tiled=True)  25 us
    another operation x15, other arithmetic  22.6 us
    div x7, other arithmetic, local(): krylov_basis.append(image / beta_norm)  20.2 us
  transfers between devices with their start and end apart: 3, of which 1 were waited for; matrix products, arithmetic and copies ran while one was open for 5% of the time, Pallas kernels for 0%

profile of v1, /device:TPU:32, one launch (start us, length us, event | category | flops | bytes accessed | tf_op | source)
XLA Modules:
  0.0 829.6 jit_solution(14678832597537749762)
XLA Ops:
  14.3 18.5 %psum.448 = f32[]{:T(128)} all-reduce(f32[]{:T(128)} %multiply_reduce_fusion.43), channel_id=1, replica_groups=mesh['grp_0'=8,'grp_1'=2,'row_0'=4,'row_1'=4] {'grp_0'}, use_global_device_ids=true, to_apply=%region_1.0 | all-reduce | flops 1 | bytes 8 | tf_op jit(solution)/shard_map/psum | solution.py:36
  35.9 44.1 %psum.450 = f32[]{:T(128)} all-reduce(f32[]{:T(128)} %psum.449), channel_id=1, replica_groups=mesh['grp_0'=8,'grp_1'=2,'row_0'=4,'row_1'=4] {'row_0'}, use_global_device_ids=true, to_apply=%region_3.0 | all-reduce | flops 1 | bytes 8 | tf_op jit(solution)/shard_map/psum | solution.py:36
  80.0 59.5 %psum.451 = f32[]{:T(128)} all-reduce(f32[]{:T(128)} %psum.450), channel_id=1, replica_groups=mesh['grp_0'=8,'grp_1'=2,'row_0'=4,'row_1'=4] {'row_1'}, use_global_device_ids=true, to_apply=%region_4.0 | all-reduce | flops 1 | bytes 8 | tf_op jit(solution)/shard_map/psum | solution.py:36
  154.0 31.6 %all_to_all.45 = f32[16,2,32,512]{3,2,1,0:T(8,128)S(1)} all-to-all(f32[16,2,32,512]{3,2,1,0:T(8,128)S(1)} %bitcast.298), channel_id=1, replica_groups=mesh['grp_0'=8,'grp_1'=2,'row_0'=4,'row_1'=4] {'row_0','row_1'}, dimensions={0} | all-to-all | bytes 4194304 | tf_op jit(solution)/shard_map/all_to_all | solution.py:31
  186.5 18.5 %all-reduce.7 = (f32[]{:T(128)}, f32[1]{0:T(128)}) all-reduce(f32[]{:T(128)} %get-tuple-element.224, f32[1]{0:T(128)} %bitcast.10), channel_id=1, replica_groups=mesh['grp_0'=8,'grp_1'=2,'row_0'=4,'row_1'=4] {'grp_0'}, use_global_device_ids=true, to_apply=%region_12.0 | all-reduce | flops 2 | bytes 16 | tf_op jit(solution)/shard_map/psum | solution.py:36
  208.1 9.2 %all-reduce.21 = (f32[]{:T(128)}, f32[1]{0:T(128)}) all-reduce(f32[]{:T(128)} %get-tuple-element.281, f32[1]{0:T(128)} %get-tuple-element.282), channel_id=1, replica_groups=mesh['grp_0'=8,'grp_1'=2,'row_0'=4,'row_1'=4] {'row_0'}, use_global_device_ids=true, to_apply=%region_14.0 | all-reduce | flops 2 | bytes 16 | tf_op jit(solution)/shard_map/psum | solution.py:36
  217.2 9.2 %all-reduce.14 = (f32[]{:T(128)}, f32[1]{0:T(128)}) all-reduce(f32[]{:T(128)} %get-tuple-element.267, f32[1]{0:T(128)} %get-tuple-element.268), channel_id=1, replica_groups=mesh['grp_0'=8,'grp_1'=2,'row_0'=4,'row_1'=4] {'row_1'}, use_global_device_ids=true, to_apply=%region_15.0 | all-reduce | flops 2 | bytes 16 | tf_op jit(solution)/shard_map/psum | solution.py:36
  234.7 27.9 %all_to_all.46 = f32[16,2,32,512]{3,2,1,0:T(8,128)S(1)} all-to-all(f32[16,2,32,512]{3,2,1,0:T(8,128)S(1)} %bitcast.299), channel_id=1, replica_groups=mesh['grp_0'=8,'grp_1'=2,'row_0'=4,'row_1'=4] {'row_0','row_1'}, dimensions={0} | all-to-all | bytes 4194304 | tf_op jit(solution)/shard_map/all_to_all | solution.py:31
  264.8 17.0 %all-reduce.6 = (f32[]{:T(128)}, f32[2]{0:T(128)S(1)}) all-reduce(f32[]{:T(128)} %get-tuple-element.222, f32[2]{0:T(128)S(1)} %pad_maximum_fusion), channel_id=1, replica_groups=mesh['grp_0'=8,'grp_1'=2,'row_0'=4,'row_1'=4] {'grp_0'}, use_global_device_ids=true, to_apply=%region_24.0 | all-reduce | flops 3 | bytes 24 | tf_op jit(solution)/shard_map/psum | solution.py:36
  284.8 9.2 %all-reduce.20 = (f32[]{:T(128)}, f32[2]{0:T(128)S(1)}) all-reduce(f32[]{:T(128)} %get-tuple-element.279, f32[2]{0:T(128)S(1)} %get-tuple-element.280), channel_id=1, replica_groups=mesh['grp_0'=8,'grp_1'=2,'row_0'=4,'row_1'=4] {'row_0'}, use_global_device_ids=true, to_apply=%region_26.0 | all-reduce | flops 3 | bytes 24 | tf_op jit(solution)/shard_map/psum | solution.py:36
  294.0 9.2 %all-reduce.13 = (f32[]{:T(128)}, f32[2]{0:T(128)S(1)}) all-reduce(f32[]{:T(128)} %get-tuple-element.265, f32[2]{0:T(128)S(1)} %get-tuple-element.266), channel_id=1, replica_groups=mesh['grp_0'=8,'grp_1'=2,'row_0'=4,'row_1'=4] {'row_1'}, use_global_device_ids=true, to_apply=%region_27.0 | all-reduce | flops 3 | bytes 24 | tf_op jit(solution)/shard_map/psum | solution.py:36
  312.5 27.9 %all_to_all.47 = f32[16,2,32,512]{3,2,1,0:T(8,128)S(1)} all-to-all(f32[16,2,32,512]{3,2,1,0:T(8,128)S(1)} %bitcast.300), channel_id=1, replica_groups=mesh['grp_0'=8,'grp_1'=2,'row_0'=4,'row_1'=4] {'row_0','row_1'}, dimensions={0} | all-to-all | bytes 4194304 | tf_op jit(solution)/shard_map/all_to_all | solution.py:31
  343.2 14.8 %all-reduce.5 = (f32[]{:T(128)}, f32[3]{0:T(128)S(1)}) all-reduce(f32[]{:T(128)} %get-tuple-element.219, f32[3]{0:T(128)S(1)} %pad_maximum_fusion.1), channel_id=1, replica_groups=mesh['grp_0'=8,'grp_1'=2,'row_0'=4,'row_1'=4] {'grp_0'}, use_global_device_ids=true, to_apply=%region_39.0 | all-reduce | flops 4 | bytes 32 | tf_op jit(solution)/shard_map/psum | solution.py:36
  361.1 9.2 %all-reduce.19 = (f32[]{:T(128)}, f32[3]{0:T(128)S(1)}) all-reduce(f32[]{:T(128)} %get-tuple-element.277, f32[3]{0:T(128)S(1)} %get-tuple-element.278), channel_id=1, replica_groups=mesh['grp_0'=8,'grp_1'=2,'row_0'=4,'row_1'=4] {'row_0'}, use_global_device_ids=true, to_apply=%region_41.0 | all-reduce | flops 4 | bytes 32 | tf_op jit(solution)/shard_map/psum | solution.py:36
  370.3 9.2 %all-reduce.12 = (f32[]{:T(128)}, f32[3]{0:T(128)S(1)}) all-reduce(f32[]{:T(128)} %get-tuple-element.263, f32[3]{0:T(128)S(1)} %get-tuple-element.264), channel_id=1, replica_groups=mesh['grp_0'=8,'grp_1'=2,'row_0'=4,'row_1'=4] {'row_1'}, use_global_device_ids=true, to_apply=%region_42.0 | all-reduce | flops 4 | bytes 32 | tf_op jit(solution)/shard_map/psum | solution.py:36
  389.4 27.9 %all_to_all.48 = f32[16,2,32,512]{3,2,1,0:T(8,128)S(1)} all-to-all(f32[16,2,32,512]{3,2,1,0:T(8,128)S(1)} %bitcast.301), channel_id=1, replica_groups=mesh['grp_0'=8,'grp_1'=2,'row_0'=4,'row_1'=4] {'row_0','row_1'}, dimensions={0} | all-to-all | bytes 4194304 | tf_op jit(solution)/shard_map/all_to_all | solution.py:31
  420.7 16.8 %all-reduce.4 = (f32[]{:T(128)}, f32[4]{0:T(128)S(1)}) all-reduce(f32[]{:T(128)} %get-tuple-element.215, f32[4]{0:T(128)S(1)} %pad_maximum_fusion.2), channel_id=1, replica_groups=mesh['grp_0'=8,'grp_1'=2,'row_0'=4,'row_1'=4] {'grp_0'}, use_global_device_ids=true, to_apply=%region_55.0 | all-reduce | flops 5 | bytes 40 | tf_op jit(solution)/shard_map/psum | solution.py:36
  440.5 9.4 %all-reduce.18 = (f32[]{:T(128)}, f32[4]{0:T(128)S(1)}) all-reduce(f32[]{:T(128)} %get-tuple-element.275, f32[4]{0:T(128)S(1)} %get-tuple-element.276), channel_id=1, replica_groups=mesh['grp_0'=8,'grp_1'=2,'row_0'=4,'row_1'=4] {'row_0'}, use_global_device_ids=true, to_apply=%region_57.0 | all-reduce | flops 5 | bytes 40 | tf_op jit(solution)/shard_map/psum | solution.py:36
  449.9 9.2 %all-reduce.11 = (f32[]{:T(128)}, f32[4]{0:T(128)S(1)}) all-reduce(f32[]{:T(128)} %get-tuple-element.261, f32[4]{0:T(128)S(1)} %get-tuple-element.262), channel_id=1, replica_groups=mesh['grp_0'=8,'grp_1'=2,'row_0'=4,'row_1'=4] {'row_1'}, use_global_device_ids=true, to_apply=%region_58.0 | all-reduce | flops 5 | bytes 40 | tf_op jit(solution)/shard_map/psum | solution.py:36
  469.5 27.9 %all_to_all.49 = f32[16,2,32,512]{3,2,1,0:T(8,128)S(1)} all-to-all(f32[16,2,32,512]{3,2,1,0:T(8,128)S(1)} %bitcast.302), channel_id=1, replica_groups=mesh['grp_0'=8,'grp_1'=2,'row_0'=4,'row_1'=4] {'row_0','row_1'}, dimensions={0} | all-to-all | bytes 4194304 | tf_op jit(solution)/shard_map/all_to_all | solution.py:31
  501.4 14.8 %all-reduce.3 = (f32[]{:T(128)}, f32[5]{0:T(128)S(1)}) all-reduce(f32[]{:T(128)} %get-tuple-element.209, f32[5]{0:T(128)S(1)} %stack.167), channel_id=1, replica_groups=mesh['grp_0'=8,'grp_1'=2,'row_0'=4,'row_1'=4] {'grp_0'}, use_global_device_ids=true, to_apply=%region_72.0 | all-reduce | flops 6 | bytes 48 | tf_op jit(solution)/shard_map/psum | solution.py:36
  519.2 9.2 %all-reduce.17 = (f32[]{:T(128)}, f32[5]{0:T(128)S(1)}) all-reduce(f32[]{:T(128)} %get-tuple-element.273, f32[5]{0:T(128)S(1)} %get-tuple-element.274), channel_id=1, replica_groups=mesh['grp_0'=8,'grp_1'=2,'row_0'=4,'row_1'=4] {'row_0'}, use_global_device_ids=true, to_apply=%region_74.0 | all-reduce | flops 6 | bytes 48 | tf_op jit(solution)/shard_map/psum | solution.py:36
  528.4 9.2 %all-reduce.10 = (f32[]{:T(128)}, f32[5]{0:T(128)S(1)}) all-reduce(f32[]{:T(128)} %get-tuple-element.259, f32[5]{0:T(128)S(1)} %get-tuple-element.260), channel_id=1, replica_groups=mesh['grp_0'=8,'grp_1'=2,'row_0'=4,'row_1'=4] {'row_1'}, use_global_device_ids=true, to_apply=%region_75.0 | all-reduce | flops 6 | bytes 48 | tf_op jit(solution)/shard_map/psum | solution.py:36
  548.8 27.9 %all_to_all.50 = f32[16,2,32,512]{3,2,1,0:T(8,128)S(1)} all-to-all(f32[16,2,32,512]{3,2,1,0:T(8,128)S(1)} %bitcast.303), channel_id=1, replica_groups=mesh['grp_0'=8,'grp_1'=2,'row_0'=4,'row_1'=4] {'row_0','row_1'}, dimensions={0} | all-to-all | bytes 4194304 | tf_op jit(solution)/shard_map/all_to_all | solution.py:31
  581.4 16.8 %all-reduce.2 = (f32[]{:T(128)}, f32[6]{0:T(128)S(1)}) all-reduce(f32[]{:T(128)} %get-tuple-element.203, f32[6]{0:T(128)S(1)} %stack.174), channel_id=1, replica_groups=mesh['grp_0'=8,'grp_1'=2,'row_0'=4,'row_1'=4] {'grp_0'}, use_global_device_ids=true, to_apply=%region_90.0 | all-reduce | flops 7 | bytes 56 | tf_op jit(solution)/shard_map/psum | solution.py:36
  601.3 9.2 %all-reduce.16 = (f32[]{:T(128)}, f32[6]{0:T(128)S(1)}) all-reduce(f32[]{:T(128)} %get-tuple-element.271, f32[6]{0:T(128)S(1)} %get-tuple-element.272), channel_id=1, replica_groups=mesh['grp_0'=8,'grp_1'=2,'row_0'=4,'row_1'=4] {'row_0'}, use_global_device_ids=true, to_apply=%region_92.0 | all-reduce | flops 7 | bytes 56 | tf_op jit(solution)/shard_map/psum | solution.py:36
  610.5 9.2 %all-reduce.9 = (f32[]{:T(128)}, f32[6]{0:T(128)S(1)}) all-reduce(f32[]{:T(128)} %get-tuple-element.257, f32[6]{0:T(128)S(1)} %get-tuple-element.258), channel_id=1, replica_groups=mesh['grp_0'=8,'grp_1'=2,'row_0'=4,'row_1'=4] {'row_1'}, use_global_device_ids=true, to_apply=%region_93.0 | all-reduce | flops 7 | bytes 56 | tf_op jit(solution)/shard_map/psum | solution.py:36
  639.8 25.0 %all-to-all-done.7 = f32[16,2,32,512]{3,2,1,0:T(8,128)S(1)} async-done(((f32[16,2,32,512]{3,2,1,0:T(8,128)}), f32[16,2,32,512]{3,2,1,0:T(8,128)S(1)}, u32[]{:S(2)}, u32[]{:S(2)}) %all-to-all-start.7) | async-done | bytes 2097184 | tf_op jit(solution)/shard_map/all_to_all | solution.py:31
  671.8 14.8 %all-reduce.1 = (f32[]{:T(128)}, f32[7]{0:T(128)S(1)}) all-reduce(f32[]{:T(128)} %get-tuple-element.196, f32[7]{0:T(128)S(1)} %stack.182), channel_id=1, replica_groups=mesh['grp_0'=8,'grp_1'=2,'row_0'=4,'row_1'=4] {'grp_0'}, use_global_device_ids=true, to_apply=%region_109.0 | all-reduce | flops 8 | bytes 64 | tf_op jit(solution)/shard_map/psum | solution.py:36
  776.3 16.1 %psum.508 = f32[8]{0:T(128)S(1)} all-reduce(f32[8]{0:T(128)S(1)} %stack.191), channel_id=1, replica_groups=mesh['grp_0'=8,'grp_1'=2,'row_0'=4,'row_1'=4] {'grp_0'}, use_global_device_ids=true, to_apply=%region_123.0 | all-reduce | flops 8 | bytes 64 | tf_op jit(solution)/shard_map/psum | solution.py:36
  798.2 10.9 %psum.510 = f32[8]{0:T(128)S(1)} all-reduce(f32[8]{0:T(128)S(1)} %psum.509), channel_id=1, replica_groups=mesh['grp_0'=8,'grp_1'=2,'row_0'=4,'row_1'=4] {'row_0'}, use_global_device_ids=true, to_apply=%region_125.0 | all-reduce | flops 8 | bytes 64 | tf_op jit(solution)/shard_map/psum | solution.py:36
  809.3 10.4 %psum.511 = f32[8,1]{1,0:T(8,128)S(1)} all-reduce(f32[8,1]{1,0:T(8,128)S(1)} %copy.35), channel_id=1, replica_groups=mesh['grp_0'=8,'grp_1'=2,'row_0'=4,'row_1'=4] {'row_1'}, use_global_device_ids=true, to_apply=%region_126.0 | all-reduce | flops 8 | bytes 64 | tf_op jit(solution)/shard_map/psum | solution.py:36
  (165 shorter events, 238.8 us)
Async XLA Ops:
  0.6 147.8 %copy-start = (bf16[2,8,32,512]{3,2,1,0:T(8,128)(2,1)S(1)}, bf16[2,8,32,512]{3,2,1,0:T(8,128)(2,1)}, u32[]{:S(2)}) copy-start(bf16[2,8,32,512]{3,2,1,0:T(8,128)(2,1)} %param.35) | copy-start | bytes 1572868
  6.0 7.2 copy-start.8
  6.0 7.6 copy-start.1
  6.0 134.2 %all-to-all-start = ((bf16[16,2,8,32,512]{4,3,2,1,0:T(8,128)(2,1)}), bf16[16,2,8,32,512]{4,3,2,1,0:T(8,128)(2,1)}, u32[]{:S(2)}, u32[]{:S(2)}) async-start(bf16[16,2,8,32,512]{4,3,2,1,0:T(8,128)(2,1)} %stack.148), calls=%async_computation | async-start | bytes 16777216 | tf_op jit(solution)/shard_map/all_to_all | solution.py:19
  303.2 2.5 copy-start.9
  379.5 2.5 copy-start.7
  459.1 2.4 copy-start.6
  537.6 39.0 %copy-start.5 = (f32[5]{0:T(128)}, f32[5]{0:T(128)S(1)}, u32[]{:S(2)}) copy-start(f32[5]{0:T(128)S(1)} %get-tuple-element.246) | copy-start | bytes 64
  576.8 45.4 %copy-start.3 = (f32[2,32,512]{2,1,0:T(8,128)}, f32[2,32,512]{2,1,0:T(8,128)S(1)}, u32[]{:S(2)}) copy-start(f32[2,32,512]{2,1,0:T(8,128)S(1)} %reduce_sum.559) | copy-start | bytes 393220
  619.7 14.1 %copy-start.4 = (f32[6]{0:T(128)}, f32[6]{0:T(128)S(1)}, u32[]{:S(2)}) copy-start(f32[6]{0:T(128)S(1)} %get-tuple-element.244) | copy-start | bytes 76
  633.8 31.0 %all-to-all-start.7 = ((f32[16,2,32,512]{3,2,1,0:T(8,128)}), f32[16,2,32,512]{3,2,1,0:T(8,128)S(1)}, u32[]{:S(2)}, u32[]{:S(2)}) async-start(f32[16,2,32,512]{3,2,1,0:T(8,128)} %bitcast.297), calls=%async_computation.7 | async-start | bytes 4194304 | tf_op jit(solution)/shard_map/all_to_all | solution.py:31
  722.7 45.8 %all-to-all-start.8 = ((f32[16,2,32,512]{3,2,1,0:T(8,128)}), f32[16,2,32,512]{3,2,1,0:T(8,128)S(1)}, u32[]{:S(2)}, u32[]{:S(2)}) async-start(f32[16,2,32,512]{3,2,1,0:T(8,128)} %bitcast.296), calls=%async_computation.8 | async-start | bytes 4194304 | tf_op jit(solution)/shard_map/all_to_all | solution.py:31
  819.8 9.8 %copy-start.2 = (f32[8,8]{1,0:T(8,128)}, f32[8,8]{1,0:T(8,128)S(1)}, u32[]{:S(2)}) copy-start(f32[8,8]{1,0:T(8,128)S(1)} %scatter.74) | copy-start | bytes 772
